TPU v7x, 16 devices: a 4x2x1 block of a 4x4x8 slice. The times are simulated.
16 devices in a mesh: rep: 4 (over y, z, core), dp: 4 (over x).
Axes of the slice: x: 4, y: 2, z: 1, core: 2. Of those that a mesh axis runs over, the one named last changes fastest.
The devices are a block of a 4x4x8 slice.
Arguments:
- g_w_gate: bfloat16 [16, 2, 1024, 4096], P(('rep', 'dp')), parts along dimension 0
- g_w_up: bfloat16 [16, 2, 1024, 4096], P(('rep', 'dp')), parts along dimension 0
- g_w_down: bfloat16 [16, 2, 4096, 1024], P(('rep', 'dp')), parts along dimension 0
- w_gate: bfloat16 [2, 1024, 4096], replicated
- w_up: bfloat16 [2, 1024, 4096], replicated
- w_down: bfloat16 [2, 4096, 1024], replicated
- m_w_gate: float32 [2, 1024, 4096], P(None, 'dp')
- m_w_up: float32 [2, 1024, 4096], P(None, 'dp')
- m_w_down: float32 [2, 4096, 1024], P(None, 'dp')
- v_w_gate: float32 [2, 1024, 4096], P(None, 'dp')
- v_w_up: float32 [2, 1024, 4096], P(None, 'dp')
- v_w_down: float32 [2, 4096, 1024], P(None, 'dp')
Outputs:
- output 1: bfloat16 [8, 1024, 4096], P('rep'), parts along dimension 0
- output 2: bfloat16 [8, 1024, 4096], P('rep'), parts along dimension 0
- output 3: bfloat16 [8, 4096, 1024], P('rep'), parts along dimension 0
- output 4: float32 [8, 1024, 4096], P('rep', 'dp'), parts along dimension 0
- output 5: float32 [8, 1024, 4096], P('rep', 'dp'), parts along dimension 0
- output 6: float32 [8, 4096, 1024], P('rep', 'dp'), parts along dimension 0
- output 7: float32 [8, 1024, 4096], P('rep', 'dp'), parts along dimension 0
- output 8: float32 [8, 1024, 4096], P('rep', 'dp'), parts along dimension 0
- output 9: float32 [8, 4096, 1024], P('rep', 'dp'), parts along dimension 0
There are 4 independent parts. A program takes and returns all parts, laid end to end along the dimension named above; an argument that names none is the same for every part.
All inputs are finite; a program needn't handle non-finite values.
Results may differ from a plain program's by a relative error of at most 0.022.
Values are sent between devices in bfloat16 or wider.
A program may use at most 768 MiB of HBM per device.

v0:
```python
import jax
import jax.numpy as jnp
from jax import lax
from jax.sharding import PartitionSpec as P


def adamw(w, m, v, g):
    m = 0.9 * m + 0.1 * g
    v = 0.95 * v + 0.05 * g * g
    step = m * lax.rsqrt(v + 1e-8) + 0.1 * w
    return (w - 0.02 * step).astype(jnp.bfloat16), m, v


def solution(mesh):
    def step(*arrays):
        terms, weights, m, v = (arrays[i : i + 3] for i in (0, 3, 6, 9))
        gradients = [lax.psum_scatter(t[0], "dp", scatter_dimension=1, tiled=True).astype(jnp.float32) for t in terms]
        me = lax.axis_index("dp")
        own = [lax.dynamic_slice_in_dim(w, me * one.shape[1], one.shape[1], 1).astype(jnp.float32) for w, one in zip(weights, m, strict=True)]
        new = [adamw(w, m, v, g) for w, m, v, g in zip(own, m, v, gradients, strict=True)]
        whole = [lax.all_gather(one[0], "dp", axis=1, tiled=True) for one in new]
        return (*whole, *(one[1] for one in new), *(one[2] for one in new))

    all_of, cut = P(None, None, None), P(None, "dp", None)
    return jax.shard_map(
        step,
        mesh=mesh,
        in_specs=(P(("rep", "dp"), None, None, None),) * 3 + (all_of,) * 3 + (cut,) * 6,
        out_specs=(P("rep", None, None),) * 3 + (P("rep", "dp", None),) * 6,
        check_vma=False,
    )
```

profile of v0, /device:TPU:112, one launch (start us, length us, event | category | flops | bytes accessed | tf_op | source)
XLA Modules:
  0.0 950.1 jit_solution(5253403763851197739)
XLA Ops:
  7.2 0.1 reduce-scatter.8.cloned.1.call-start
  7.3 0.7 reduce-scatter.8.cloned.1.call-update
  8.0 0.1 reduce-scatter.6.cloned.1.call-start
  8.1 0.7 reduce-scatter.6.cloned.1.call-update
  8.8 0.1 reduce-scatter.4.cloned.1.call-start
  8.9 0.7 reduce-scatter.4.cloned.1.call-update
  9.6 0.1 all-gather.8.cloned.1.call-start
  9.7 147.5 %reduce-scatter.8.cloned.1.call-done = bf16[2,1024,1024]{2,1,0:T(8,128)(2,1)} async-done(((bf16[2,4096,1024]{2,1,0:T(8,128)(2,1)}), bf16[2,1024,1024]{2,1,0:T(8,128)(2,1)}) %reduce-scatter.8.cloned.1.call-update) | async-done | bytes 4194320 | tf_op jit(solution)/shard_map/reduce_scatter | solution.py:17
  157.2 16.9 %fusion.10 = (bf16[2,1024,1024]{2,1,0:T(8,128)(2,1)}, f32[2,1024,1024]{2,1,0:T(8,128)}, f32[2,1024,1024]{2,1,0:T(8,128)}) fusion(bf16[2,4096,1024]{2,1,0:T(8,128)(2,1)} %param.17, s32[]{:T(128)S(6)} %select_n.8, bf16[2,1024,1024]{2,1,0:T(8,128)(2,1)} %reduce-scatter.8.cloned.1.call-done, f32[2,1024,1024]{2,1,0:T(8,128)} %param.23, f32[2,1024,1024]{2,1,0:T(8,128)} %param.20), kind=kLoop, calls=%fused_computation.22 | loop fusion | flops 33554432 | bytes 46137348 | tf_op jit(solution)/shard_map/convert_element_type | solution.py:11
  174.0 0.1 all-gather.8.cloned.1.call-update
  174.1 0.1 all-gather.6.cloned.1.call-start
  174.2 128.9 %reduce-scatter.6.cloned.1.call-done = bf16[2,256,4096]{2,1,0:T(8,128)(2,1)} async-done(((bf16[2,1024,4096]{2,1,0:T(8,128)(2,1)}), bf16[2,256,4096]{2,1,0:T(8,128)(2,1)}) %reduce-scatter.6.cloned.1.call-update) | async-done | bytes 4194320 | tf_op jit(solution)/shard_map/reduce_scatter | solution.py:17
  303.1 17.1 %fusion.6 = (bf16[2,256,4096]{2,1,0:T(8,128)(2,1)}, f32[2,256,4096]{2,1,0:T(8,128)}, f32[2,256,4096]{2,1,0:T(8,128)}) fusion(bf16[2,1024,4096]{2,1,0:T(8,128)(2,1)} %param.16, s32[]{:T(128)S(6)} %select_n.7, bf16[2,256,4096]{2,1,0:T(8,128)(2,1)} %reduce-scatter.6.cloned.1.call-done, f32[2,256,4096]{2,1,0:T(8,128)} %param.22, f32[2,256,4096]{2,1,0:T(8,128)} %param.19), kind=kLoop, calls=%fused_computation.18 | loop fusion | flops 33554432 | bytes 46137348 | tf_op jit(solution)/shard_map/convert_element_type | solution.py:11
  320.2 0.1 all-gather.6.cloned.1.call-update
  320.3 0.1 all-gather.4.cloned.1.call-start
  320.4 128.7 %reduce-scatter.4.cloned.1.call-done = bf16[2,256,4096]{2,1,0:T(8,128)(2,1)} async-done(((bf16[2,1024,4096]{2,1,0:T(8,128)(2,1)}), bf16[2,256,4096]{2,1,0:T(8,128)(2,1)}) %reduce-scatter.4.cloned.1.call-update) | async-done | bytes 4194320 | tf_op jit(solution)/shard_map/reduce_scatter | solution.py:17
  449.1 17.1 %fusion.2 = (bf16[2,256,4096]{2,1,0:T(8,128)(2,1)}, f32[2,256,4096]{2,1,0:T(8,128)}, f32[2,256,4096]{2,1,0:T(8,128)}) fusion(bf16[2,1024,4096]{2,1,0:T(8,128)(2,1)} %param.15, s32[]{:T(128)S(6)} %select_n.7, bf16[2,256,4096]{2,1,0:T(8,128)(2,1)} %reduce-scatter.4.cloned.1.call-done, f32[2,256,4096]{2,1,0:T(8,128)} %param.21, f32[2,256,4096]{2,1,0:T(8,128)} %param.18), kind=kLoop, calls=%fused_computation.14 | loop fusion | flops 33554432 | bytes 46137348 | tf_op jit(solution)/shard_map/convert_element_type | solution.py:11
  466.2 0.1 all-gather.4.cloned.1.call-update
  466.3 135.4 %all-gather.8.cloned.1.call-done = bf16[2,4096,1024]{2,1,0:T(8,128)(2,1)} async-done(((bf16[2,1024,1024]{2,1,0:T(8,128)(2,1)}), bf16[2,4096,1024]{2,1,0:T(8,128)(2,1)}) %all-gather.8.cloned.1.call-update) | async-done | bytes 16777232 | tf_op jit(solution)/shard_map/all_gather | solution.py:21
  601.6 153.7 %all-gather.6.cloned.1.call-done = bf16[2,1024,4096]{2,1,0:T(8,128)(2,1)} async-done(((bf16[2,256,4096]{2,1,0:T(8,128)(2,1)}), bf16[2,1024,4096]{2,1,0:T(8,128)(2,1)}) %all-gather.6.cloned.1.call-update) | async-done | bytes 16777232 | tf_op jit(solution)/shard_map/all_gather | solution.py:21
  755.4 153.8 %all-gather.4.cloned.1.call-done = bf16[2,1024,4096]{2,1,0:T(8,128)(2,1)} async-done(((bf16[2,256,4096]{2,1,0:T(8,128)(2,1)}), bf16[2,1024,4096]{2,1,0:T(8,128)(2,1)}) %all-gather.4.cloned.1.call-update) | async-done | bytes 16777232 | tf_op jit(solution)/shard_map/all_gather | solution.py:21
  909.1 0.0 copy-start
  909.1 0.0 slice-start
  909.1 0.0 slice-start.1
  909.1 16.8 %copy.24 = bf16[2,1024,4096]{2,1,0:T(8,128)(2,1)} copy(bf16[2,1024,4096]{2,1,0:T(8,128)(2,1)} %all-gather.4.cloned.1.call-done) | data formatting | bytes 33554432
  925.9 0.0 copy-done
  925.9 8.5 copy.25
  934.4 0.0 slice-done
  934.4 0.0 slice-done.1
  934.4 1.4 slice-done.2
  935.9 1.2 slice-done.3
  937.1 6.2 copy.26
  (3 shorter events, 0.0 us)
Async XLA Ops:
  7.2 150.0 %reduce-scatter.8.cloned.1.call-start = ((), (), s32[]{:S(2)}) async-start(), calls=%async_computation.7 | async-start | bytes 20971520 | tf_op jit(solution)/shard_map/reduce_scatter | solution.py:17
  8.0 295.1 %reduce-scatter.6.cloned.1.call-start = ((), (), s32[]{:S(2)}) async-start(), calls=%async_computation.5 | async-start | bytes 20971520 | tf_op jit(solution)/shard_map/reduce_scatter | solution.py:17
  8.8 440.3 %reduce-scatter.4.cloned.1.call-start = ((), (), s32[]{:S(2)}) async-start(), calls=%async_computation.3 | async-start | bytes 20971520 | tf_op jit(solution)/shard_map/reduce_scatter | solution.py:17
  9.6 592.1 %all-gather.8.cloned.1.call-start = ((), (), s32[]{:S(2)}) async-start(), calls=%async_computation.8 | async-start | bytes 20971520 | tf_op jit(solution)/shard_map/all_gather | solution.py:21
  174.1 581.3 %all-gather.6.cloned.1.call-start = ((), (), s32[]{:S(2)}) async-start(), calls=%async_computation.6 | async-start | bytes 20971520 | tf_op jit(solution)/shard_map/all_gather | solution.py:21
  320.3 588.8 %all-gather.4.cloned.1.call-start = ((), (), s32[]{:S(2)}) async-start(), calls=%async_computation.4 | async-start | bytes 20971520 | tf_op jit(solution)/shard_map/all_gather | solution.py:21
  909.1 16.8 %copy-start = (bf16[2,1024,4096]{2,1,0:T(8,128)(2,1)S(1)}, bf16[2,1024,4096]{2,1,0:T(8,128)(2,1)}, u32[]{:S(2)}) copy-start(bf16[2,1024,4096]{2,1,0:T(8,128)(2,1)} %all-gather.6.cloned.1.call-done) | copy-start | bytes 50331652
  909.1 25.3 %slice-start = ((s8[16777216]{0:T(1024)(128)(4,1)}), s8[4194304]{0:T(1024)(128)(4,1)S(1)}, s32[]{:S(2)}) async-start(s8[16777216]{0:T(1024)(128)(4,1)} %bitcast.6), calls=%async_computation.9 | async-start | bytes 8388608
  909.1 25.3 %slice-start.1 = ((s8[16777216]{0:T(1024)(128)(4,1)}), s8[4194304]{0:T(1024)(128)(4,1)S(1)}, s32[]{:S(2)}) async-start(s8[16777216]{0:T(1024)(128)(4,1)} %bitcast.6), calls=%async_computation.10 | async-start | bytes 8388608
  925.9 9.9 %slice-start.2 = ((s8[16777216]{0:T(1024)(128)(4,1)}), s8[4194304]{0:T(1024)(128)(4,1)S(1)}, s32[]{:S(2)}) async-start(s8[16777216]{0:T(1024)(128)(4,1)} %bitcast.6), calls=%async_computation.11 | async-start | bytes 8388608
  925.9 11.1 %slice-start.3 = ((s8[16777216]{0:T(1024)(128)(4,1)}), s8[4194304]{0:T(1024)(128)(4,1)S(1)}, s32[]{:S(2)}) async-start(s8[16777216]{0:T(1024)(128)(4,1)} %bitcast.6), calls=%async_computation.12 | async-start | bytes 8388608
Sparse Core Ops, SparseCore 0:
  10.4 146.7 reduce-scatter.7
  159.5 143.5 reduce-scatter.5
  305.5 143.5 reduce-scatter.3
  451.1 150.5 all-gather.7
  603.6 151.7 all-gather.5
  757.4 151.7 all-gather.3
where the time goes:
time: 950 us
  waiting for transfers between devices  850 us (89%)
  other arithmetic  51.1 us (5%)
  local copies, waits for them, and re-layouts  34.1 us (4%)
  between operations  14.2 us (1%)
    all_gather x3, waiting for transfers between devices, step(): whole = [lax.all_gather(one[0], 'dp', axis=1, tiled=True) for one in new]  443 us
    reduce_scatter x3, waiting for transfers between devices, step(): lax.psum_scatter(t[0], 'dp', scatter_dimension=1, tiled=True)  405 us
    convert_element_type x3, other arithmetic, adamw(): return ((w - 0.02 * step).astype(jnp.bfloat16), m, v)  51.1 us
    unnamed x13, local copies, waits for them, and re-layouts  34.1 us
  transfers between devices with their start and end apart: 6, of which 6 were waited for; matrix products, arithmetic and copies ran while one was open for 5% of the time, Pallas kernels for 0%

commit v1 on v0

v1 whole, which is shorter than its diff:
```python
import functools

import jax
import jax.numpy as jnp
from jax import lax
from jax.experimental import pallas as pl
from jax.experimental.pallas import tpu as pltpu
from jax.sharding import PartitionSpec as P

MESH = pl.DeviceIdType.MESH
ROWS, COLS = 256, 1024
RIGHT, LEFT = 0, 1
STRIP = 32
LATER = 3
VMEM_LIMIT = 67043328


def adamw(w, m, v, g):
    m = 0.9 * m + 0.1 * g
    v = 0.95 * v + 0.05 * g * g
    step = m * lax.rsqrt(v + 1e-8) + 0.1 * w
    return (w - 0.02 * step).astype(jnp.bfloat16), m, v


class Pieces:
    def __init__(self, block):
        self.layers, self.rows, cols = block
        self.across = cols // COLS
        self.each = (self.rows // ROWS) * self.across
        assert self.rows % ROWS == 0 and cols % COLS == 0 and self.each % 2 == 0

    def of(self, ref, layer, owner, q):
        start = pl.multiple_of(owner * self.rows + (q // self.across) * ROWS, ROWS)
        return ref.at[layer, pl.ds(start, ROWS), pl.ds((q % self.across) * COLS, COLS)]


def kernel(lay, *refs):
    grads, weights, ms, vs, sums, gathered = (refs[i : i + 3] for i in range(0, 18, 3))
    onward = refs[18:20]
    (
        hop, got, own_b, g_b, w_b, m_b, v_b, sum_b, new_b,
        s1_send, s1_recv, s2_send, s2_recv, a1_send, a1_recv, a2_send, a2_recv,
        own_sem, in_sem, out_sem,
    ) = refs[20:]
    n = lax.axis_size("dp")
    me = lax.axis_index("dp")
    rep = lax.axis_index("rep")
    right, left, across = lax.rem(me + 1, n), lax.rem(me + n - 1, n), lax.rem(me + 2, n)
    to = (right, left)
    came = (left, right)

    units = [(i, layer) for i in range(3) for layer in range(lay[i].layers)]
    each = lay[0].each
    half = each // 2
    halves = (range(0, half), range(half, each))

    def remote(src, dst, sends, recvs, d, k):
        return pltpu.make_async_remote_copy(
            src_ref=src,
            dst_ref=dst,
            send_sem=sends.at[d, k],
            recv_sem=recvs.at[d, k],
            device_id=(rep, to[d]),
            device_id_type=MESH,
        )

    def piece(arrays, u, owner, q):
        i, layer = units[u]
        return lay[i].of(arrays[i], layer, owner, q)

    def first(d, u, j):
        return remote(piece(grads, u, across, halves[d][j]), hop.at[d, u * half + j], s1_send, s1_recv, d, u * half + j)

    def plain(d, u, j):
        q = halves[1 - d][j]
        return remote(piece(grads, u, to[d], q), got.at[d, u * each + q], s2_send, s2_recv, d, u * each + q)

    def added(d, u, j):
        q = halves[d][j]
        return remote(hop.at[d, u * half + j], got.at[d, u * each + q], s2_send, s2_recv, d, u * each + q)

    def out(d, u, q):
        src = piece(gathered, u, me, q)
        return remote(src, src, a1_send, a1_recv, d, u * each + q)

    def on(d, u, j):
        src = piece(gathered, u, came[d], halves[d][j])
        return remote(src, src, a2_send, a2_recv, d, u * half + j)

    barrier = pltpu.get_barrier_semaphore()
    for device in to:
        pl.semaphore_signal(barrier, inc=1, device_id=(rep, device), device_id_type=MESH)

    many = range(len(units))
    adds = [(d, u, j) for u in many for j in range(half) for d in (RIGHT, LEFT)]
    steps = [(u, q) for u in many for q in range(each)]

    def own_load(k):
        d, u, j = adds[k]
        return pltpu.make_async_copy(piece(grads, u, to[d], halves[d][j]), own_b.at[k % 2], own_sem.at[k % 2])

    def loads(k):
        u, q = steps[k]
        s = k % 2
        i, layer = units[u]
        return [
            pltpu.make_async_copy(src, dst.at[s], in_sem.at[a, s])
            for a, (src, dst) in enumerate(
                (
                    (piece(grads, u, me, q), g_b),
                    (piece(weights, u, me, q), w_b),
                    (lay[i].of(ms[i], layer, 0, q), m_b),
                    (lay[i].of(vs[i], layer, 0, q), v_b),
                )
            )
        ]

    def store_new(k):
        u, q = steps[k]
        return pltpu.make_async_copy(new_b.at[k % 2], piece(gathered, u, me, q), out_sem.at[0, k % 2])

    def store_sum(k):
        u, q = steps[k]
        i, layer = units[u]
        return pltpu.make_async_copy(sum_b.at[k % 2], lay[i].of(sums[i], layer, 0, q), out_sem.at[1, k % 2])

    own_load(0).start()
    for copy in loads(0):
        copy.start()

    pl.semaphore_wait(barrier, 2)
    for u in many:
        for j in range(half):
            for d in (RIGHT, LEFT):
                first(d, u, j).start()
    for u in many:
        for j in range(half):
            for d in (RIGHT, LEFT):
                plain(d, u, j).start()

    for k, (d, u, j) in enumerate(adds):
        if k + 1 < len(adds):
            own_load(k + 1).start()
        own_load(k).wait()
        first(d, u, j).wait_recv()

        @pl.loop(0, ROWS // STRIP)
        def _(t, d=d, u=u, j=j, k=k):
            at = pl.ds(pl.multiple_of(t * STRIP, STRIP), STRIP)
            mine = own_b[k % 2, at, :].astype(jnp.float32)
            hop[d, u * half + j, at, :] = (hop[d, u * half + j, at, :].astype(jnp.float32) + mine).astype(jnp.bfloat16)

        added(d, u, j).start()

    def send_out(k):
        u, q = steps[k]
        store_new(k).wait()
        for d in (RIGHT, LEFT):
            out(d, u, q).start()

    for k, (u, q) in enumerate(steps):
        s = k % 2
        if k + 1 < len(steps):
            for copy in loads(k + 1):
                copy.start()
        for copy in loads(k):
            copy.wait()
        for d in (RIGHT, LEFT):
            plain(d, u, q % half).wait_recv() if q in halves[1 - d] else added(d, u, q % half).wait_recv()
        if k >= 2:
            store_sum(k - 2).wait()

        @pl.loop(0, ROWS // STRIP)
        def _(t, s=s, k=k):
            at = pl.ds(pl.multiple_of(t * STRIP, STRIP), STRIP)
            g = g_b[s, at, :].astype(jnp.float32) + got[RIGHT, k, at, :].astype(jnp.float32)
            g = (g + got[LEFT, k, at, :].astype(jnp.float32)).astype(jnp.bfloat16)
            sum_b[s, at, :] = g
            new_b[s, at, :] = adamw(w_b[s, at, :].astype(jnp.float32), m_b[s, at, :], v_b[s, at, :], g.astype(jnp.float32))[0]

        store_new(k).start()
        store_sum(k).start()
        if k >= 1:
            send_out(k - 1)
    last = len(steps) - 1
    send_out(last)
    store_sum(last - 1).wait()
    store_sum(last).wait()

    k = 0
    for u in range(LATER):
        for j in range(half):
            for d in (RIGHT, LEFT):
                out(d, u, halves[d][j]).wait_recv()
                bounce = own_b.at[k % 2]
                take = pltpu.make_async_copy(piece(gathered, u, came[d], halves[d][j]), bounce, own_sem.at[k % 2])
                take.start()
                take.wait()
                put = pltpu.make_async_copy(bounce, onward[d].at[u * half + j], own_sem.at[k % 2])
                put.start()
                put.wait()
                k += 1
    for u in many[LATER:]:
        for j in range(half):
            for d in (RIGHT, LEFT):
                out(d, u, halves[d][j]).wait_recv()
                on(d, u, j).start()

    for d in (RIGHT, LEFT):
        for u in many:
            for j in range(half):
                first(d, u, j).wait_send()
                plain(d, u, j).wait_send()
                added(d, u, j).wait_send()
                out(d, u, halves[1 - d][j]).wait_recv()
                if u >= LATER:
                    on(d, u, j).wait()
            for q in range(each):
                out(d, u, q).wait_send()


def spread(lay, *refs):
    brought, wholes = refs[:2], refs[2:5]
    outs, buf, in_sem, out_sem = refs[5:8], refs[8], refs[9], refs[10]
    del wholes
    n = lax.axis_size("dp")
    across = lax.rem(lax.axis_index("dp") + 2, n)
    units = [(i, layer) for i in range(3) for layer in range(lay[i].layers)]
    each = lay[0].each
    half = each // 2
    copies = []
    for d in (RIGHT, LEFT):
        for u in range(LATER):
            for j in range(half):
                i, layer = units[u]
                q = j + d * half
                k = len(copies)
                copies.append(
                    (
                        pltpu.make_async_copy(brought[d].at[u * half + j], buf.at[k], in_sem.at[k]),
                        pltpu.make_async_copy(buf.at[k], lay[i].of(outs[i], layer, across, q), out_sem.at[k]),
                    )
                )
    for take, _ in copies:
        take.start()
    for take, put in copies:
        take.wait()
        put.start()
    for _, put in copies:
        put.wait()


def settle(src, dst):
    dst[...] = src[...]


def settled(x):
    layers, rows, cols = x.shape
    step = (1 << 20) // cols
    spec = pl.BlockSpec((1, step, cols), lambda i, j: (i, j, 0))
    return pl.pallas_call(
        settle,
        grid=(layers, rows // step),
        in_specs=[spec],
        out_specs=spec,
        out_shape=jax.ShapeDtypeStruct(x.shape, x.dtype),
        cost_estimate=pl.CostEstimate(flops=x.size * 40, bytes_accessed=4 * x.size, transcendentals=0),
        name="settle",
    )(x)


def solution(mesh):
    def step(*arrays):
        terms, weights, m, v = (arrays[i : i + 3] for i in (0, 3, 6, 9))
        lay = [Pieces(one.shape) for one in m]
        each = lay[0].each
        assert all(one.each == each for one in lay) and mesh.shape["dp"] == 4
        units = sum(one.layers for one in lay)
        half = each // 2
        anywhere = pl.BlockSpec(memory_space=pl.ANY)
        bf16 = jnp.bfloat16
        dma = pltpu.SemaphoreType.DMA
        res = pl.pallas_call(
            functools.partial(kernel, lay),
            out_shape=[jax.ShapeDtypeStruct(one.shape, bf16) for one in m]
            + [jax.ShapeDtypeStruct(one.shape, bf16) for one in weights]
            + [jax.ShapeDtypeStruct((LATER * half, ROWS, COLS), bf16)] * 2,
            in_specs=[anywhere] * 12,
            out_specs=[anywhere] * 8,
            scratch_shapes=[
                pltpu.VMEM((2, units * half, ROWS, COLS), bf16),
                pltpu.VMEM((2, units * each, ROWS, COLS), bf16),
                pltpu.VMEM((2, ROWS, COLS), bf16),
                pltpu.VMEM((2, ROWS, COLS), bf16),
                pltpu.VMEM((2, ROWS, COLS), bf16),
                pltpu.VMEM((2, ROWS, COLS), jnp.float32),
                pltpu.VMEM((2, ROWS, COLS), jnp.float32),
                pltpu.VMEM((2, ROWS, COLS), bf16),
                pltpu.VMEM((2, ROWS, COLS), bf16),
                dma((2, units * half)), dma((2, units * half)),
                dma((2, units * each)), dma((2, units * each)),
                dma((2, units * each)), dma((2, units * each)),
                dma((2, units * half)), dma((2, units * half)),
                dma((2,)), dma((4, 2)), dma((2, 2)),
            ],
            compiler_params=pltpu.CompilerParams(collective_id=0, has_side_effects=True, vmem_limit_bytes=VMEM_LIMIT),
            name="sum_step_gather",
        )(*(t[0] for t in terms), *weights, *m, *v)
        sums, gathered, onward = res[:3], res[3:6], res[6:8]
        n = mesh.shape["dp"]
        brought = [
            lax.ppermute(onward[RIGHT], "dp", [(i, (i + 1) % n) for i in range(n)]),
            lax.ppermute(onward[LEFT], "dp", [(i, (i - 1) % n) for i in range(n)]),
        ]
        wholes = [settled(one) for one in gathered]
        new_m, new_v = [], []
        for one_m, one_v, g in zip(m, v, sums, strict=True):
            g = g.astype(jnp.float32)
            new_m.append(0.9 * one_m + 0.1 * g)
            new_v.append(0.95 * one_v + 0.05 * g * g)
        pieces = 2 * LATER * half
        wholes = pl.pallas_call(
            functools.partial(spread, lay),
            out_shape=[jax.ShapeDtypeStruct(one.shape, one.dtype) for one in wholes],
            in_specs=[anywhere] * 5,
            out_specs=[anywhere] * 3,
            input_output_aliases={2: 0, 3: 1, 4: 2},
            scratch_shapes=[pltpu.VMEM((pieces, ROWS, COLS), bf16), dma((pieces,)), dma((pieces,))],
            name="spread",
        )(*brought, *wholes)
        return (*wholes, *new_m, *new_v)

    all_of, cut = P(None, None, None), P(None, "dp", None)
    return jax.shard_map(
        step,
        mesh=mesh,
        in_specs=(P(("rep", "dp"), None, None, None),) * 3 + (all_of,) * 3 + (cut,) * 6,
        out_specs=(P("rep", None, None),) * 3 + (P("rep", "dp", None),) * 6,
        check_vma=False,
    )
```

time: 950 us -> 842 us (0.89)
  waiting for transfers between devices: 850 us -> 0.01 us
  Pallas kernels: 0 us -> 796 us
  local copies, waits for them, and re-layouts: 34.1 us -> 1.63 us
  between operations: 14.2 us -> 0.67 us
  other arithmetic: 51.1 us -> 38.8 us
    pallas_call x0 -> x5, Pallas kernels: none -> 796 us  [the longest x1 749 us: step(): pl.pallas_call(functools.partial(kernel, lay), out_shape=[jax.ShapeDtypeS...]
    all_gather x3 -> x0, waiting for transfers between devices: 443 us -> none  [step(): whole = [lax.all_gather(one[0], 'dp', axis=1, tiled=True) for one in new]]
    reduce_scatter x3 -> x0, waiting for transfers between devices: 405 us -> none  [step(): lax.psum_scatter(t[0], 'dp', scatter_dimension=1, tiled=True)]
    convert_element_type x3 -> x0, other arithmetic: 51.1 us -> none  [adamw(): return ((w - 0.02 * step).astype(jnp.bfloat16), m, v)]
    add x0 -> x2, other arithmetic: none -> 38.8 us  [step(): new_v.append(0.95 * one_v + 0.05 * g * g)]
    unnamed x13 -> x2, local copies, waits for them, and re-layouts: 34.1 us -> 1.63 us
  transfers between devices with their start and end apart: 6 -> 2, of which waited for: 6 -> 0; matrix products, arithmetic and copies ran while one was open for 5% -> 5% of each run, Pallas kernels for 0% -> 5%
where the time goes in v1:
time: 842 us; the launch traced here: 841 us
  Pallas kernels  796 us (95%)
  other arithmetic  38.8 us (5%)
    pallas_call x1, Pallas kernels, step(): pl.pallas_call(functools.partial(kernel, lay), out_shape=[jax.ShapeDtypeS...  749 us
    pallas_call x3, Pallas kernels, settled(): pl.pallas_call(settle, grid=(layers, rows // step), in_specs=[spec], out_...  41.4 us
    add x2, other arithmetic, step(): new_v.append(0.95 * one_v + 0.05 * g * g)  38.8 us
  transfers between devices with their start and end apart: 2, of which 0 were waited for; matrix products, arithmetic and copies ran while one was open for 5% of the time, Pallas kernels for 5%

profile of v1, /device:TPU:112, one launch (start us, length us, event | category | flops | bytes accessed | tf_op | source)
XLA Modules:
  0.0 840.7 jit_solution(851200095055903909)
XLA Ops:
  0.6 749.5 %sum_step_gather.1 = (bf16[2,256,4096]{2,1,0:T(8,128)(2,1)}, bf16[2,256,4096]{2,1,0:T(8,128)(2,1)}, bf16[2,1024,1024]{2,1,0:T(8,128)(2,1)}, bf16[2,1024,4096]{2,...) custom-call(bf16[2,1024,4096]{2,1,0:T(8,128)(2,1)} %bitcast.3, ...), custom_call_target="tpu_custom_call" | custom-call | tf_op jit(solution)/shard_map/sum_step_gather/pallas_call | solution.py:283
  750.1 1.4 collective-permute-start
  751.5 1.9 collective-permute-start.1
  753.4 12.5 %fusion.5 = (f32[2,1024,1024]{2,1,0:T(8,128)}, f32[2,1024,1024]{2,1,0:T(8,128)}) fusion(bf16[2,1024,1024]{2,1,0:T(8,128)(2,1)} %get-tuple-element.30, f32[2,1024,1024]{2,1,0:T(8,128)} %refs_11_.1, f32[2,1024,1024]{2,1,0:T(8,128)} %refs_8_.1), kind=kLoop, calls=%fused_computation.11 | loop fusion | flops 16777216 | bytes 37748736 | tf_op jit(solution)/shard_map/add | solution.py:320
  765.9 13.8 %settle.3.refs_2_ = bf16[2,1024,4096]{2,1,0:T(8,128)(2,1)} custom-call(bf16[2,1024,4096]{2,1,0:T(8,128)(2,1)} %get-tuple-element.22.src), custom_call_target="tpu_custom_call" | custom-call | flops 335544320 | bytes 33554432 | tf_op jit(solution)/shard_map/settle/pallas_call | solution.py:261
  779.7 13.8 %settle.4.refs_3_ = bf16[2,1024,4096]{2,1,0:T(8,128)(2,1)} custom-call(bf16[2,1024,4096]{2,1,0:T(8,128)(2,1)} %get-tuple-element.23.src), custom_call_target="tpu_custom_call" | custom-call | flops 335544320 | bytes 33554432 | tf_op jit(solution)/shard_map/settle/pallas_call | solution.py:261
  793.5 13.8 %settle.5.refs_4_ = bf16[2,4096,1024]{2,1,0:T(8,128)(2,1)} custom-call(bf16[2,4096,1024]{2,1,0:T(8,128)(2,1)} %get-tuple-element.24.src), custom_call_target="tpu_custom_call" | custom-call | flops 335544320 | bytes 33554432 | tf_op jit(solution)/shard_map/settle/pallas_call | solution.py:261
  807.3 26.3 %fusion.3 = (f32[2,256,4096]{2,1,0:T(8,128)}, f32[2,256,4096]{2,1,0:T(8,128)}, f32[2,256,4096]{2,1,0:T(8,128)}, f32[2,256,4096]{2,1,0:T(8,128)}) fusion(bf16[2,256,4096]{2,1,0:T(8,128)(2,1)} %get-tuple-element.28, f32[2,256,4096]{2,1,0:T(8,128)} %refs_9_.1, f32[2,256,4096]{2,1,0:T(8,128)} %refs_6_.1, bf16[2,256,4096]{2,1,0:T(8,128)(2,1)} %get-tuple-element.29, ...), kind=kLoop, calls=%fused_computation.9 | loop fusion | flops 33554432 | bytes 75497472 | tf_op jit(solution)/shard_map/add | solution.py:320
  833.6 0.0 collective-permute-done.refs_0_
  833.6 0.0 copy-start
  833.6 0.0 collective-permute-done.1.refs_1_
  833.6 1.6 copy-done
  835.3 5.5 spread.1
Async XLA Ops:
  750.1 83.5 %collective-permute-start = (bf16[6,256,1024]{2,1,0:T(8,128)(2,1)}, bf16[6,256,1024]{2,1,0:T(8,128)(2,1)S(1)}, u32[]{:S(2)}, u32[]{:S(2)}) collective-permute-start(bf16[6,256,1024]{2,1,0:T(8,128)(2,1)} %get-tuple-element.20), channel_id=1, source_target_pairs={{0,1},{1,2},{2,3},{3,0},{4,5},{5,6},{6,7},{7,4},{8,9},{9,10},{10,1... | collective-permute-start | bytes 9437192 | tf_op jit(solution)/shard_map/ppermute | solution.py:312
  751.5 82.1 %collective-permute-start.1 = (bf16[6,256,1024]{2,1,0:T(8,128)(2,1)}, bf16[6,256,1024]{2,1,0:T(8,128)(2,1)}, u32[]{:S(2)}, u32[]{:S(2)}) collective-permute-start(bf16[6,256,1024]{2,1,0:T(8,128)(2,1)} %get-tuple-element.21), channel_id=1, source_target_pairs={{0,3},{1,0},{2,1},{3,2},{4,7},{5,4},{6,5},{7,6},{8,11},{9,8},{10,9... | collective-permute-start | bytes 9437192 | tf_op jit(solution)/shard_map/ppermute | solution.py:313
  833.6 1.7 copy-start

commit v2 on v1

--- a/solution.py
+++ b/solution.py
@@ -7,11 +7,13 @@
 from jax.experimental.pallas import tpu as pltpu
 from jax.sharding import PartitionSpec as P
 
+
 MESH = pl.DeviceIdType.MESH
 ROWS, COLS = 256, 1024
 RIGHT, LEFT = 0, 1
 STRIP = 32
-LATER = 3
+LATER = 4
+LAST = 1
 VMEM_LIMIT = 67043328
 
 
@@ -36,12 +38,12 @@
 
 def kernel(lay, *refs):
     grads, weights, ms, vs, sums, gathered = (refs[i : i + 3] for i in range(0, 18, 3))
-    onward = refs[18:20]
+    onward = refs[18:22]
     (
         hop, got, own_b, g_b, w_b, m_b, v_b, sum_b, new_b,
         s1_send, s1_recv, s2_send, s2_recv, a1_send, a1_recv, a2_send, a2_recv,
         own_sem, in_sem, out_sem,
-    ) = refs[20:]
+    ) = refs[22:]
     n = lax.axis_size("dp")
     me = lax.axis_index("dp")
     rep = lax.axis_index("rep")
@@ -187,19 +189,19 @@
     store_sum(last - 1).wait()
     store_sum(last).wait()
 
-    k = 0
+    split = LATER * half - LAST
     for u in range(LATER):
         for j in range(half):
             for d in (RIGHT, LEFT):
+                k = u * half + j
                 out(d, u, halves[d][j]).wait_recv()
-                bounce = own_b.at[k % 2]
-                take = pltpu.make_async_copy(piece(gathered, u, came[d], halves[d][j]), bounce, own_sem.at[k % 2])
+                take = pltpu.make_async_copy(piece(gathered, u, came[d], halves[d][j]), own_b.at[d], own_sem.at[d])
                 take.start()
                 take.wait()
-                put = pltpu.make_async_copy(bounce, onward[d].at[u * half + j], own_sem.at[k % 2])
+                dst = onward[d].at[k] if k < split else onward[2 + d].at[k - split]
+                put = pltpu.make_async_copy(own_b.at[d], dst, own_sem.at[d])
                 put.start()
                 put.wait()
-                k += 1
     for u in many[LATER:]:
         for j in range(half):
             for d in (RIGHT, LEFT):
@@ -219,35 +221,22 @@
                 out(d, u, q).wait_send()
 
 
-def spread(lay, *refs):
-    brought, wholes = refs[:2], refs[2:5]
-    outs, buf, in_sem, out_sem = refs[5:8], refs[8], refs[9], refs[10]
-    del wholes
+def spread(lay, first, *refs):
+    brought, outs, sem = refs[:2], refs[5:8], refs[8]
     n = lax.axis_size("dp")
     across = lax.rem(lax.axis_index("dp") + 2, n)
     units = [(i, layer) for i in range(3) for layer in range(lay[i].layers)]
-    each = lay[0].each
-    half = each // 2
+    half = lay[0].each // 2
     copies = []
     for d in (RIGHT, LEFT):
-        for u in range(LATER):
-            for j in range(half):
-                i, layer = units[u]
-                q = j + d * half
-                k = len(copies)
-                copies.append(
-                    (
-                        pltpu.make_async_copy(brought[d].at[u * half + j], buf.at[k], in_sem.at[k]),
-                        pltpu.make_async_copy(buf.at[k], lay[i].of(outs[i], layer, across, q), out_sem.at[k]),
-                    )
-                )
-    for take, _ in copies:
-        take.start()
-    for take, put in copies:
-        take.wait()
-        put.start()
-    for _, put in copies:
-        put.wait()
+        for k in range(brought[d].shape[0]):
+            i, layer = units[(first + k) // half]
+            q = (first + k) % half + d * half
+            copies.append(pltpu.make_async_copy(brought[d].at[k], lay[i].of(outs[i], layer, across, q), sem.at[len(copies)]))
+    for copy in copies:
+        copy.start()
+    for copy in copies:
+        copy.wait()
 
 
 def settle(src, dst):
@@ -284,9 +273,10 @@
             functools.partial(kernel, lay),
             out_shape=[jax.ShapeDtypeStruct(one.shape, bf16) for one in m]
             + [jax.ShapeDtypeStruct(one.shape, bf16) for one in weights]
-            + [jax.ShapeDtypeStruct((LATER * half, ROWS, COLS), bf16)] * 2,
+            + [jax.ShapeDtypeStruct((LATER * half - LAST, ROWS, COLS), bf16)] * 2
+            + [jax.ShapeDtypeStruct((LAST, ROWS, COLS), bf16)] * 2,
             in_specs=[anywhere] * 12,
-            out_specs=[anywhere] * 8,
+            out_specs=[anywhere] * 10,
             scratch_shapes=[
                 pltpu.VMEM((2, units * half, ROWS, COLS), bf16),
                 pltpu.VMEM((2, units * each, ROWS, COLS), bf16),
@@ -306,28 +296,29 @@
             compiler_params=pltpu.CompilerParams(collective_id=0, has_side_effects=True, vmem_limit_bytes=VMEM_LIMIT),
             name="sum_step_gather",
         )(*(t[0] for t in terms), *weights, *m, *v)
-        sums, gathered, onward = res[:3], res[3:6], res[6:8]
+        sums, gathered, onward = res[:3], res[3:6], res[6:10]
         n = mesh.shape["dp"]
-        brought = [
-            lax.ppermute(onward[RIGHT], "dp", [(i, (i + 1) % n) for i in range(n)]),
-            lax.ppermute(onward[LEFT], "dp", [(i, (i - 1) % n) for i in range(n)]),
-        ]
+        brought = []
+        for k in (0, 2):
+            for x, hop in zip(onward[k : k + 2], (1, -1), strict=True):
+                brought.append(lax.ppermute(x, "dp", [(i, (i + hop) % n) for i in range(n)]))
         wholes = [settled(one) for one in gathered]
         new_m, new_v = [], []
         for one_m, one_v, g in zip(m, v, sums, strict=True):
             g = g.astype(jnp.float32)
             new_m.append(0.9 * one_m + 0.1 * g)
             new_v.append(0.95 * one_v + 0.05 * g * g)
-        pieces = 2 * LATER * half
-        wholes = pl.pallas_call(
-            functools.partial(spread, lay),
-            out_shape=[jax.ShapeDtypeStruct(one.shape, one.dtype) for one in wholes],
-            in_specs=[anywhere] * 5,
-            out_specs=[anywhere] * 3,
-            input_output_aliases={2: 0, 3: 1, 4: 2},
-            scratch_shapes=[pltpu.VMEM((pieces, ROWS, COLS), bf16), dma((pieces,)), dma((pieces,))],
-            name="spread",
-        )(*brought, *wholes)
+        for pair, first in ((brought[:2], 0), (brought[2:], LATER * half - LAST)):
+            wholes = pl.pallas_call(
+                functools.partial(spread, lay, first),
+                out_shape=[jax.ShapeDtypeStruct(one.shape, one.dtype) for one in wholes],
+                in_specs=[pl.BlockSpec(memory_space=pltpu.VMEM)] * 2 + [anywhere] * 3,
+                out_specs=[anywhere] * 3,
+                input_output_aliases={2: 0, 3: 1, 4: 2},
+                scratch_shapes=[dma((2 * pair[0].shape[0],))],
+                compiler_params=pltpu.CompilerParams(vmem_limit_bytes=24 << 20),
+                name="spread",
+            )(*pair, *wholes)
         return (*wholes, *new_m, *new_v)
 
     all_of, cut = P(None, None, None), P(None, "dp", None)

time: 842 us -> 830 us (0.986)
  Pallas kernels: 796 us -> 776 us
    pallas_call x1, Pallas kernels: 749 us -> 727 us  [step(): pl.pallas_call(functools.partial(kernel, lay), out_shape=[jax.ShapeDtypeS...]
  transfers between devices with their start and end apart: 2 -> 4, of which waited for: 0 -> 1; matrix products, arithmetic and copies ran while one was open for 5% -> 4% of each run, Pallas kernels for 5% -> 6%
where the time goes in v2:
time: 830 us; the launch traced here: 828 us
  Pallas kernels  776 us (93%)
  other arithmetic  36.6 us (4%)
    pallas_call x1, Pallas kernels, step(): pl.pallas_call(functools.partial(kernel, lay), out_shape=[jax.ShapeDtypeS...  727 us
    pallas_call x3, Pallas kernels, settled(): pl.pallas_call(settle, grid=(layers, rows // step), in_specs=[spec], out_...  41.4 us
    add x2, other arithmetic, step(): new_v.append(0.95 * one_v + 0.05 * g * g)  36.6 us
  transfers between devices with their start and end apart: 4, of which 1 were waited for; matrix products, arithmetic and copies ran while one was open for 4% of the time, Pallas kernels for 6%

profile of v2, /device:TPU:112, one launch (start us, length us, event | category | flops | bytes accessed | tf_op | source)
XLA Modules:
  0.0 828.4 jit_solution(18078116278680011785)
XLA Ops:
  0.6 727.3 %sum_step_gather.1 = (bf16[2,256,4096]{2,1,0:T(8,128)(2,1)}, bf16[2,256,4096]{2,1,0:T(8,128)(2,1)}, bf16[2,1024,1024]{2,1,0:T(8,128)(2,1)}, bf16[2,1024,4096]{2,...) custom-call(bf16[2,1024,4096]{2,1,0:T(8,128)(2,1)} %bitcast.3, ...), custom_call_target="tpu_custom_call" | custom-call | tf_op jit(solution)/shard_map/sum_step_gather/pallas_call | solution.py:272
  728.0 1.4 collective-permute-start
  729.4 1.9 collective-permute-start.1
  731.3 0.1 collective-permute-start.2
  731.4 3.1 collective-permute-start.3
  734.5 0.0 copy-start
  734.5 0.0 copy-start.1
  734.5 26.9 %fusion.3 = (f32[2,256,4096]{2,1,0:T(8,128)}, f32[2,256,4096]{2,1,0:T(8,128)}, f32[2,256,4096]{2,1,0:T(8,128)}, f32[2,256,4096]{2,1,0:T(8,128)}) fusion(bf16[2,256,4096]{2,1,0:T(8,128)(2,1)} %get-tuple-element.38, f32[2,256,4096]{2,1,0:T(8,128)} %refs_9_.1, f32[2,256,4096]{2,1,0:T(8,128)} %refs_6_.1, bf16[2,256,4096]{2,1,0:T(8,128)(2,1)} %get-tuple-element.39, ...), kind=kLoop, calls=%fused_computation.9 | loop fusion | flops 33554432 | bytes 75497472 | tf_op jit(solution)/shard_map/add | solution.py:310
  761.4 0.0 copy-done
  761.4 1.6 copy-done.1
  763.0 9.8 %fusion.5 = (f32[2,1024,1024]{2,1,0:T(8,128)}, f32[2,1024,1024]{2,1,0:T(8,128)}) fusion(bf16[2,1024,1024]{2,1,0:T(8,128)(2,1)S(1)} %copy-done.1, f32[2,1024,1024]{2,1,0:T(8,128)} %refs_11_.1, f32[2,1024,1024]{2,1,0:T(8,128)S(1)} %copy-done), kind=kLoop, calls=%fused_computation.11 | loop fusion | flops 16777216 | bytes 37748736 | tf_op jit(solution)/shard_map/add | solution.py:310
  772.7 13.8 %settle.3.refs_2_ = bf16[2,1024,4096]{2,1,0:T(8,128)(2,1)} custom-call(bf16[2,1024,4096]{2,1,0:T(8,128)(2,1)} %get-tuple-element.29.src), custom_call_target="tpu_custom_call" | custom-call | flops 335544320 | bytes 33554432 | tf_op jit(solution)/shard_map/settle/pallas_call | solution.py:250
  786.5 13.8 %settle.4.refs_3_ = bf16[2,1024,4096]{2,1,0:T(8,128)(2,1)} custom-call(bf16[2,1024,4096]{2,1,0:T(8,128)(2,1)} %get-tuple-element.30.src), custom_call_target="tpu_custom_call" | custom-call | flops 335544320 | bytes 33554432 | tf_op jit(solution)/shard_map/settle/pallas_call | solution.py:250
  800.3 13.8 %settle.5.refs_4_ = bf16[2,4096,1024]{2,1,0:T(8,128)(2,1)} custom-call(bf16[2,4096,1024]{2,1,0:T(8,128)(2,1)} %get-tuple-element.31.src), custom_call_target="tpu_custom_call" | custom-call | flops 335544320 | bytes 33554432 | tf_op jit(solution)/shard_map/settle/pallas_call | solution.py:250
  814.1 7.0 collective-permute-done.2.refs_0_
  821.1 0.0 collective-permute-done.3.refs_1_
  821.1 6.2 spread.2
  827.3 0.0 collective-permute-done.refs_0_
  827.4 0.0 collective-permute-done.1.refs_1_
  827.4 1.0 spread.3
Async XLA Ops:
  728.0 99.4 %collective-permute-start = (bf16[1,256,1024]{2,1,0:T(8,128)(2,1)}, bf16[1,256,1024]{2,1,0:T(8,128)(2,1)S(1)}, u32[]{:S(2)}, u32[]{:S(2)}) collective-permute-start(bf16[1,256,1024]{2,1,0:T(8,128)(2,1)} %get-tuple-element.25), channel_id=1, source_target_pairs={{0,1},{1,2},{2,3},{3,0},{4,5},{5,6},{6,7},{7,4},{8,9},{9,10},{10,1... | collective-permute-start | bytes 1572872 | tf_op jit(solution)/shard_map/ppermute | solution.py:304
  729.4 98.0 %collective-permute-start.1 = (bf16[1,256,1024]{2,1,0:T(8,128)(2,1)}, bf16[1,256,1024]{2,1,0:T(8,128)(2,1)S(1)}, u32[]{:S(2)}, u32[]{:S(2)}) collective-permute-start(bf16[1,256,1024]{2,1,0:T(8,128)(2,1)} %get-tuple-element.26), channel_id=1, source_target_pairs={{0,3},{1,0},{2,1},{3,2},{4,7},{5,4},{6,5},{7,6},{8,11},{9,8},{10,9... | collective-permute-start | bytes 1572872 | tf_op jit(solution)/shard_map/ppermute | solution.py:304
  731.3 89.8 %collective-permute-start.2 = (bf16[7,256,1024]{2,1,0:T(8,128)(2,1)}, bf16[7,256,1024]{2,1,0:T(8,128)(2,1)}, u32[]{:S(2)}, u32[]{:S(2)}) collective-permute-start(bf16[7,256,1024]{2,1,0:T(8,128)(2,1)} %get-tuple-element.27), channel_id=1, source_target_pairs={{0,1},{1,2},{2,3},{3,0},{4,5},{5,6},{6,7},{7,4},{8,9},{9,10},{10,1... | collective-permute-start | bytes 11010056 | tf_op jit(solution)/shard_map/ppermute | solution.py:304
  731.4 89.7 %collective-permute-start.3 = (bf16[7,256,1024]{2,1,0:T(8,128)(2,1)}, bf16[7,256,1024]{2,1,0:T(8,128)(2,1)}, u32[]{:S(2)}, u32[]{:S(2)}) collective-permute-start(bf16[7,256,1024]{2,1,0:T(8,128)(2,1)} %get-tuple-element.28), channel_id=1, source_target_pairs={{0,3},{1,0},{2,1},{3,2},{4,7},{5,4},{6,5},{7,6},{8,11},{9,8},{10,9... | collective-permute-start | bytes 11010056 | tf_op jit(solution)/shard_map/ppermute | solution.py:304
  734.5 26.9 %copy-start = (f32[2,1024,1024]{2,1,0:T(8,128)S(1)}, f32[2,1024,1024]{2,1,0:T(8,128)}, u32[]{:S(2)}) copy-start(f32[2,1024,1024]{2,1,0:T(8,128)} %refs_8_.1) | copy-start | bytes 25165828
  734.5 28.4 %copy-start.1 = (bf16[2,1024,1024]{2,1,0:T(8,128)(2,1)S(1)}, bf16[2,1024,1024]{2,1,0:T(8,128)(2,1)}, u32[]{:S(2)}) copy-start(bf16[2,1024,1024]{2,1,0:T(8,128)(2,1)} %get-tuple-element.40) | copy-start | bytes 12582916

commit v3 on v2

v3 whole, which is shorter than its diff:
```python
import functools

import jax
import jax.numpy as jnp
from jax import lax
from jax.experimental import pallas as pl
from jax.experimental.pallas import tpu as pltpu
from jax.sharding import PartitionSpec as P


MESH = pl.DeviceIdType.MESH
ROWS, COLS = 256, 1024
RIGHT, LEFT = 0, 1
STRIP = 32
LATER = 4
LAST = 1
PAUSE = 10
FLIGHT = 32
VMEM_LIMIT = 67043328


def adamw(w, m, v, g):
    m = 0.9 * m + 0.1 * g
    v = 0.95 * v + 0.05 * g * g
    step = m * lax.rsqrt(v + 1e-8) + 0.1 * w
    return (w - 0.02 * step).astype(jnp.bfloat16), m, v


class Lay:
    def __init__(self, block):
        self.layers, self.rows, self.cols = block
        self.across = self.cols // COLS
        tiles = (self.rows // ROWS) * self.across
        assert self.rows % ROWS == 0 and self.cols % COLS == 0 and tiles % 2 == 0
        assert self.across == 1 or self.rows == ROWS
        self.tiles = tiles // 2
        self.half = (self.rows // 2, self.cols) if self.across == 1 else (self.rows, self.cols // 2)

    def of(self, ref, layer, owner, h):
        down, over = (h, 0) if self.across == 1 else (0, h)
        start = pl.multiple_of(owner * self.rows + down * self.half[0], ROWS)
        return ref.at[layer, pl.ds(start, self.half[0]), pl.ds(over * self.half[1], self.half[1])]

    def tile(self, ref, layer, owner, h, t):
        q = h * self.tiles + t
        start = pl.multiple_of(owner * self.rows + (q // self.across) * ROWS, ROWS)
        return ref.at[layer, pl.ds(start, ROWS), pl.ds((q % self.across) * COLS, COLS)]

    def inside(self, t, strip):
        down, over = (t, 0) if self.across == 1 else (0, t)
        return pl.ds(pl.multiple_of(down * ROWS + strip * STRIP, STRIP), STRIP), pl.ds(over * COLS, COLS)


def kernel(lay, *refs):
    grads, weights, ms, vs, sums, gathered = (refs[i : i + 3] for i in range(0, 18, 3))
    onward, hop, got = refs[18:22], refs[22:25], refs[25:28]
    (
        own_b, g_b, w_b, m_b, v_b, sum_b, new_b,
        s1_send, s1_recv, s2_send, s2_recv, a1_send, a1_recv, a2_send, a2_recv,
        own_sem, in_sem, out_sem,
    ) = refs[28:]
    n = lax.axis_size("dp")
    me = lax.axis_index("dp")
    rep = lax.axis_index("rep")
    right, left, across = lax.rem(me + 1, n), lax.rem(me + n - 1, n), lax.rem(me + 2, n)
    to = (right, left)
    came = (left, right)
    units = [(i, layer) for i in range(3) for layer in range(lay[i].layers)]
    many = range(len(units))
    tiles = lay[0].tiles
    ways = (RIGHT, LEFT)

    def remote(src, dst, sends, recvs, d, k):
        return pltpu.make_async_remote_copy(
            src_ref=src,
            dst_ref=dst,
            send_sem=sends.at[d, k],
            recv_sem=recvs.at[d, k],
            device_id=(rep, to[d]),
            device_id_type=MESH,
        )

    def part(arrays, u, owner, h):
        i, layer = units[u]
        return lay[i].of(arrays[i], layer, owner, h)

    def tile(arrays, u, owner, h, t):
        i, layer = units[u]
        return lay[i].tile(arrays[i], layer, owner, h, t)

    def first(d, u):
        i, layer = units[u]
        return remote(part(grads, u, across, d), hop[i].at[d, layer], s1_send, s1_recv, d, u)

    def plain(d, u):
        i, layer = units[u]
        return remote(part(grads, u, to[d], 1 - d), got[i].at[d, layer, 1 - d], s2_send, s2_recv, d, 2 * u + 1 - d)

    def added(d, u):
        i, layer = units[u]
        return remote(hop[i].at[d, layer], got[i].at[d, layer, d], s2_send, s2_recv, d, 2 * u + d)

    def out(d, u, h):
        src = part(gathered, u, me, h)
        return remote(src, src, a1_send, a1_recv, d, 2 * u + h)

    def on(d, u):
        src = part(gathered, u, came[d], d)
        return remote(src, src, a2_send, a2_recv, d, u)

    barrier = pltpu.get_barrier_semaphore()
    for device in to:
        pl.semaphore_signal(barrier, inc=1, device_id=(rep, device), device_id_type=MESH)

    adds = [(d, u, t) for u in many for d in ways for t in range(tiles)]
    steps = [(u, h, t) for u in many for h in range(2) for t in range(tiles)]

    def own_load(k):
        d, u, t = adds[k]
        return pltpu.make_async_copy(tile(grads, u, to[d], d, t), own_b.at[k % 2], own_sem.at[k % 2])

    def loads(k):
        u, h, t = steps[k]
        s = k % 2
        pairs = ((tile(grads, u, me, h, t), g_b), (tile(weights, u, me, h, t), w_b), (tile(ms, u, 0, h, t), m_b), (tile(vs, u, 0, h, t), v_b))
        return [pltpu.make_async_copy(src, dst.at[s], in_sem.at[a, s]) for a, (src, dst) in enumerate(pairs)]

    def store_new(k):
        u, h, t = steps[k]
        return pltpu.make_async_copy(new_b.at[k % 2], tile(gathered, u, me, h, t), out_sem.at[0, k % 2])

    def store_sum(k):
        u, h, t = steps[k]
        return pltpu.make_async_copy(sum_b.at[k % 2], tile(sums, u, 0, h, t), out_sem.at[1, k % 2])

    own_load(0).start()
    for copy in loads(0):
        copy.start()

    pl.semaphore_wait(barrier, 2)

    @pl.when(lax.rem(rep, 2) == 1)
    def _():
        @pl.loop(0, PAUSE)
        def _(_):
            pause = pltpu.make_async_copy(tile(weights, 0, me, 0, 0), new_b.at[0], own_sem.at[1])
            pause.start()
            pause.wait()

    for u in many:
        for d in ways:
            first(d, u).start()
    for u in many:
        for d in ways:
            plain(d, u).start()

    for k, (d, u, t) in enumerate(adds):
        i, layer = units[u]
        if k + 1 < len(adds):
            own_load(k + 1).start()
        own_load(k).wait()
        if t == 0:
            first(d, u).wait_recv()

        @pl.loop(0, ROWS // STRIP)
        def _(strip, d=d, i=i, layer=layer, t=t, k=k):
            at = pl.ds(pl.multiple_of(strip * STRIP, STRIP), STRIP)
            there = (d, layer, *lay[i].inside(t, strip))
            hop[i][there] = (hop[i][there].astype(jnp.float32) + own_b[k % 2, at, :].astype(jnp.float32)).astype(jnp.bfloat16)

        if t == tiles - 1:
            added(d, u).start()

    def send_out(k):
        u, h, t = steps[k]
        store_new(k).wait()
        if t == tiles - 1:
            for d in ways:
                out(d, u, h).start()

    for k, (u, h, t) in enumerate(steps):
        s = k % 2
        i, layer = units[u]
        if k + 1 < len(steps):
            for copy in loads(k + 1):
                copy.start()
        for copy in loads(k):
            copy.wait()
        if t == 0:
            for d in ways:
                (added if d == h else plain)(d, u).wait_recv()
        if k >= 2:
            store_sum(k - 2).wait()

        @pl.loop(0, ROWS // STRIP)
        def _(strip, s=s, i=i, layer=layer, h=h, t=t):
            at = pl.ds(pl.multiple_of(strip * STRIP, STRIP), STRIP)
            there = (layer, h, *lay[i].inside(t, strip))
            g = g_b[s, at, :].astype(jnp.float32) + got[i][(RIGHT, *there)].astype(jnp.float32)
            g = (g + got[i][(LEFT, *there)].astype(jnp.float32)).astype(jnp.bfloat16)
            sum_b[s, at, :] = g
            new_b[s, at, :] = adamw(w_b[s, at, :].astype(jnp.float32), m_b[s, at, :], v_b[s, at, :], g.astype(jnp.float32))[0]

        store_new(k).start()
        store_sum(k).start()
        if k >= 1:
            send_out(k - 1)
    end = len(steps) - 1
    send_out(end)
    store_sum(end - 1).wait()
    store_sum(end).wait()

    split = LATER * tiles - LAST
    for u in range(LATER):
        for d in ways:
            out(d, u, d).wait_recv()
            for t in range(tiles):
                k = u * tiles + t
                take = pltpu.make_async_copy(tile(gathered, u, came[d], d, t), own_b.at[d], own_sem.at[d])
                take.start()
                take.wait()
                dst = onward[d].at[k] if k < split else onward[2 + d].at[k - split]
                put = pltpu.make_async_copy(own_b.at[d], dst, own_sem.at[d])
                put.start()
                put.wait()
    for u in many[LATER:]:
        for d in ways:
            out(d, u, d).wait_recv()
            on(d, u).start()

    for u in many:
        for d in ways:
            first(d, u).wait_send()
            plain(d, u).wait_send()
            added(d, u).wait_send()
            out(d, u, 1 - d).wait_recv()
            for h in range(2):
                out(d, u, h).wait_send()
            if u >= LATER:
                on(d, u).wait()


def settle(lay, *refs):
    ins, outs, buf, in_sem, out_sem = refs[:3], refs[3:6], refs[6], refs[7], refs[8]
    n = lax.axis_size("dp")
    me = lax.axis_index("dp")
    units = [(i, layer) for i in range(3) for layer in range(lay[i].layers)]
    tiles = [
        (i, layer, lax.rem(me + hops, n), h, t)
        for u, (i, layer) in enumerate(units)
        for hops in range(4)
        for h in range(2)
        for t in range(lay[i].tiles)
        if hops != 2 or u >= LATER
    ]

    def take(k):
        i, *where = tiles[k]
        return pltpu.make_async_copy(lay[i].tile(ins[i], *where), buf.at[k % FLIGHT], in_sem.at[k % FLIGHT])

    def put(k):
        i, *where = tiles[k]
        return pltpu.make_async_copy(buf.at[k % FLIGHT], lay[i].tile(outs[i], *where), out_sem.at[k % FLIGHT])

    lag = FLIGHT // 2
    for k in range(len(tiles) + lag):
        if k < len(tiles):
            if k >= FLIGHT:
                put(k - FLIGHT).wait()
            take(k).start()
        if k >= lag:
            take(k - lag).wait()
            put(k - lag).start()
    for k in range(len(tiles) - FLIGHT, len(tiles)):
        put(k).wait()


def spread(lay, first, *refs):
    brought, outs, sem = refs[:2], refs[5:8], refs[8]
    n = lax.axis_size("dp")
    across = lax.rem(lax.axis_index("dp") + 2, n)
    units = [(i, layer) for i in range(3) for layer in range(lay[i].layers)]
    tiles = lay[0].tiles
    copies = []
    for d in (RIGHT, LEFT):
        for k in range(brought[d].shape[0]):
            i, layer = units[(first + k) // tiles]
            dst = lay[i].tile(outs[i], layer, across, d, (first + k) % tiles)
            copies.append(pltpu.make_async_copy(brought[d].at[k], dst, sem.at[len(copies)]))
    for copy in copies:
        copy.start()
    for copy in copies:
        copy.wait()


def solution(mesh):
    def step(*arrays):
        terms, weights, m, v = (arrays[i : i + 3] for i in (0, 3, 6, 9))
        lay = [Lay(one.shape) for one in m]
        tiles = lay[0].tiles
        assert all(one.tiles == tiles for one in lay) and mesh.shape["dp"] == 4
        units = sum(one.layers for one in lay)
        anywhere = pl.BlockSpec(memory_space=pl.ANY)
        bf16 = jnp.bfloat16
        dma = pltpu.SemaphoreType.DMA
        res = pl.pallas_call(
            functools.partial(kernel, lay),
            out_shape=[jax.ShapeDtypeStruct(one.shape, bf16) for one in m]
            + [jax.ShapeDtypeStruct(one.shape, bf16) for one in weights]
            + [jax.ShapeDtypeStruct((LATER * tiles - LAST, ROWS, COLS), bf16)] * 2
            + [jax.ShapeDtypeStruct((LAST, ROWS, COLS), bf16)] * 2,
            in_specs=[anywhere] * 12,
            out_specs=[anywhere] * 10,
            scratch_shapes=[
                *(pltpu.VMEM((2, one.layers, *one.half), bf16) for one in lay),
                *(pltpu.VMEM((2, one.layers, 2, *one.half), bf16) for one in lay),
                pltpu.VMEM((2, ROWS, COLS), bf16),
                pltpu.VMEM((2, ROWS, COLS), bf16),
                pltpu.VMEM((2, ROWS, COLS), bf16),
                pltpu.VMEM((2, ROWS, COLS), jnp.float32),
                pltpu.VMEM((2, ROWS, COLS), jnp.float32),
                pltpu.VMEM((2, ROWS, COLS), bf16),
                pltpu.VMEM((2, ROWS, COLS), bf16),
                dma((2, units)), dma((2, units)),
                dma((2, 2 * units)), dma((2, 2 * units)),
                dma((2, 2 * units)), dma((2, 2 * units)),
                dma((2, units)), dma((2, units)),
                dma((2,)), dma((4, 2)), dma((2, 2)),
            ],
            compiler_params=pltpu.CompilerParams(collective_id=0, has_side_effects=True, vmem_limit_bytes=VMEM_LIMIT),
            name="sum_step_gather",
        )(*(t[0] for t in terms), *weights, *m, *v)
        sums, gathered, onward = res[:3], res[3:6], res[6:10]
        n = mesh.shape["dp"]
        brought = []
        for k in (0, 2):
            for x, hop in zip(onward[k : k + 2], (1, -1), strict=True):
                brought.append(lax.ppermute(x, "dp", [(i, (i + hop) % n) for i in range(n)]))
        size = sum(one.size for one in gathered)
        wholes = pl.pallas_call(
            functools.partial(settle, lay),
            out_shape=[jax.ShapeDtypeStruct(one.shape, one.dtype) for one in gathered],
            in_specs=[anywhere] * 3,
            out_specs=[anywhere] * 3,
            scratch_shapes=[pltpu.VMEM((FLIGHT, ROWS, COLS), bf16), dma((FLIGHT,)), dma((FLIGHT,))],
            compiler_params=pltpu.CompilerParams(vmem_limit_bytes=54 << 20),
            cost_estimate=pl.CostEstimate(flops=size * 40, bytes_accessed=4 * size, transcendentals=0),
            name="settle",
        )(*gathered)
        new_m, new_v = [], []
        for one_m, one_v, g in zip(m, v, sums, strict=True):
            g = g.astype(jnp.float32)
            new_m.append(0.9 * one_m + 0.1 * g)
            new_v.append(0.95 * one_v + 0.05 * g * g)
        for pair, first in ((brought[:2], 0), (brought[2:], LATER * tiles - LAST)):
            wholes = pl.pallas_call(
                functools.partial(spread, lay, first),
                out_shape=[jax.ShapeDtypeStruct(one.shape, one.dtype) for one in wholes],
                in_specs=[pl.BlockSpec(memory_space=pltpu.VMEM)] * 2 + [anywhere] * 3,
                out_specs=[anywhere] * 3,
                input_output_aliases={2: 0, 3: 1, 4: 2},
                scratch_shapes=[dma((2 * pair[0].shape[0],))],
                compiler_params=pltpu.CompilerParams(vmem_limit_bytes=24 << 20),
                name="spread",
            )(*pair, *wholes)
        return (*wholes, *new_m, *new_v)

    all_of, cut = P(None, None, None), P(None, "dp", None)
    return jax.shard_map(
        step,
        mesh=mesh,
        in_specs=(P(("rep", "dp"), None, None, None),) * 3 + (all_of,) * 3 + (cut,) * 6,
        out_specs=(P("rep", None, None),) * 3 + (P("rep", "dp", None),) * 6,
        check_vma=False,
    )
```

time: 830 us -> 819 us (0.987); the launches traced: 828 us -> 808 us
  Pallas kernels: 776 us -> 749 us
    pallas_call x3 -> x1, Pallas kernels: 41.4 us -> 27.9 us  [step(): pl.pallas_call(functools.partial(settle, lay), out_shape=[jax.ShapeDtypeS...]
    pallas_call x1, Pallas kernels: 727 us -> 717 us  [step(): pl.pallas_call(functools.partial(kernel, lay), out_shape=[jax.ShapeDtypeS...]
  transfers between devices with their start and end apart: 4 -> 4, of which waited for: 1 -> 2; matrix products, arithmetic and copies ran while one was open for 4% -> 5% of each run, Pallas kernels for 6% -> 4%
where the time goes in v3:
time: 819 us; the launch traced here: 808 us
  Pallas kernels  749 us (91%)
  other arithmetic  36.8 us (4%)
  waiting for transfers between devices  14.9 us (2%)
    pallas_call x1, Pallas kernels, step(): pl.pallas_call(functools.partial(kernel, lay), out_shape=[jax.ShapeDtypeS...  717 us
    add x2, other arithmetic, step(): new_v.append(0.95 * one_v + 0.05 * g * g)  36.8 us
    pallas_call x1, Pallas kernels, step(): pl.pallas_call(functools.partial(settle, lay), out_shape=[jax.ShapeDtypeS...  27.9 us
  transfers between devices with their start and end apart: 4, of which 2 were waited for; matrix products, arithmetic and copies ran while one was open for 5% of the time, Pallas kernels for 4%

profile of v3, /device:TPU:112, one launch (start us, length us, event | category | flops | bytes accessed | tf_op | source)
XLA Modules:
  0.0 807.9 jit_solution(17032021086261353773)
XLA Ops:
  0.6 716.9 %sum_step_gather.1 = (bf16[2,256,4096]{2,1,0:T(8,128)(2,1)}, bf16[2,256,4096]{2,1,0:T(8,128)(2,1)}, bf16[2,1024,1024]{2,1,0:T(8,128)(2,1)}, bf16[2,1024,4096]{2,...) custom-call(bf16[2,1024,4096]{2,1,0:T(8,128)(2,1)} %bitcast.3, ...), custom_call_target="tpu_custom_call" | custom-call | tf_op jit(solution)/shard_map/sum_step_gather/pallas_call | solution.py:306
  717.5 2.2 collective-permute-start.2
  719.7 1.3 collective-permute-start.3
  721.0 0.7 collective-permute-start
  721.7 2.5 collective-permute-start.1
  724.2 0.0 copy-start
  724.2 26.4 %fusion.3 = (f32[2,256,4096]{2,1,0:T(8,128)}, f32[2,256,4096]{2,1,0:T(8,128)}, f32[2,256,4096]{2,1,0:T(8,128)}, f32[2,256,4096]{2,1,0:T(8,128)}) fusion(bf16[2,256,4096]{2,1,0:T(8,128)(2,1)} %get-tuple-element.44, f32[2,256,4096]{2,1,0:T(8,128)} %refs_9_.1, f32[2,256,4096]{2,1,0:T(8,128)} %refs_6_.1, bf16[2,256,4096]{2,1,0:T(8,128)(2,1)} %get-tuple-element.45, ...), kind=kLoop, calls=%fused_computation.9 | loop fusion | flops 33554432 | bytes 75497472 | tf_op jit(solution)/shard_map/add | solution.py:354
  750.7 0.0 copy-done
  750.7 10.4 %fusion.5 = (f32[2,1024,1024]{2,1,0:T(8,128)}, f32[2,1024,1024]{2,1,0:T(8,128)}) fusion(bf16[2,1024,1024]{2,1,0:T(8,128)(2,1)} %get-tuple-element.46, f32[2,1024,1024]{2,1,0:T(8,128)} %refs_11_.1, f32[2,1024,1024]{2,1,0:T(8,128)S(1)} %copy-done), kind=kLoop, calls=%fused_computation.11 | loop fusion | flops 16777216 | bytes 37748736 | tf_op jit(solution)/shard_map/add | solution.py:354
  761.1 27.9 %settle.1 = (bf16[2,1024,4096]{2,1,0:T(8,128)(2,1)}, bf16[2,1024,4096]{2,1,0:T(8,128)(2,1)}, bf16[2,4096,1024]{2,1,0:T(8,128)(2,1)}) custom-call(bf16[2,1024,4096]{2,1,0:T(8,128)(2,1)} %get-tuple-element.32.refs_0_, bf16[2,1024,4096]{2,1,0:T(8,128)(2,1)} %get-tuple-element.33.refs_1_, bf16[2,4096,1024]{2,1,0:T(8,128)(2,1)} %get-tuple-element.34.refs_2_), custom_call_target="tpu_custom_call" | custom-call | flops 1006632960 | bytes 100663296 | tf_op jit(solution)/shard_map/settle/pallas_call | solution.py:340
  789.0 6.7 collective-permute-done.2.refs_0_
  795.7 0.0 collective-permute-done.3.refs_1_
  795.7 3.1 spread.2
  798.8 8.1 %collective-permute-done.refs_0_ = bf16[1,256,1024]{2,1,0:T(8,128)(2,1)S(1)} collective-permute-done((bf16[1,256,1024]{2,1,0:T(8,128)(2,1)}, bf16[1,256,1024]{2,1,0:T(8,128)(2,1)S(1)}, u32[]{:S(2)}, u32[]{:S(2)}) %collective-permute-start) | collective-permute-done | bytes 524320 | tf_op jit(solution)/shard_map/ppermute | solution.py:338
  806.9 0.0 collective-permute-done.1.refs_1_
  806.9 1.0 spread.3
Async XLA Ops:
  717.5 78.2 %collective-permute-start.2 = (bf16[7,256,1024]{2,1,0:T(8,128)(2,1)}, bf16[7,256,1024]{2,1,0:T(8,128)(2,1)S(1)}, u32[]{:S(2)}, u32[]{:S(2)}) collective-permute-start(bf16[7,256,1024]{2,1,0:T(8,128)(2,1)} %get-tuple-element.30), channel_id=1, source_target_pairs={{0,1},{1,2},{2,3},{3,0},{4,5},{5,6},{6,7},{7,4},{8,9},{9,10},{10,1... | collective-permute-start | bytes 11010056 | tf_op jit(solution)/shard_map/ppermute | solution.py:338
  719.7 76.0 %collective-permute-start.3 = (bf16[7,256,1024]{2,1,0:T(8,128)(2,1)}, bf16[7,256,1024]{2,1,0:T(8,128)(2,1)S(1)}, u32[]{:S(2)}, u32[]{:S(2)}) collective-permute-start(bf16[7,256,1024]{2,1,0:T(8,128)(2,1)} %get-tuple-element.31), channel_id=1, source_target_pairs={{0,3},{1,0},{2,1},{3,2},{4,7},{5,4},{6,5},{7,6},{8,11},{9,8},{10,9... | collective-permute-start | bytes 11010056 | tf_op jit(solution)/shard_map/ppermute | solution.py:338
  721.0 85.9 %collective-permute-start = (bf16[1,256,1024]{2,1,0:T(8,128)(2,1)}, bf16[1,256,1024]{2,1,0:T(8,128)(2,1)S(1)}, u32[]{:S(2)}, u32[]{:S(2)}) collective-permute-start(bf16[1,256,1024]{2,1,0:T(8,128)(2,1)} %get-tuple-element.28), channel_id=1, source_target_pairs={{0,1},{1,2},{2,3},{3,0},{4,5},{5,6},{6,7},{7,4},{8,9},{9,10},{10,1... | collective-permute-start | bytes 1572872 | tf_op jit(solution)/shard_map/ppermute | solution.py:338
  721.7 85.2 %collective-permute-start.1 = (bf16[1,256,1024]{2,1,0:T(8,128)(2,1)}, bf16[1,256,1024]{2,1,0:T(8,128)(2,1)S(1)}, u32[]{:S(2)}, u32[]{:S(2)}) collective-permute-start(bf16[1,256,1024]{2,1,0:T(8,128)(2,1)} %get-tuple-element.29), channel_id=1, source_target_pairs={{0,3},{1,0},{2,1},{3,2},{4,7},{5,4},{6,5},{7,6},{8,11},{9,8},{10,9... | collective-permute-start | bytes 1572872 | tf_op jit(solution)/shard_map/ppermute | solution.py:338
  724.2 26.4 %copy-start = (f32[2,1024,1024]{2,1,0:T(8,128)S(1)}, f32[2,1024,1024]{2,1,0:T(8,128)}, u32[]{:S(2)}) copy-start(f32[2,1024,1024]{2,1,0:T(8,128)} %refs_8_.1) | copy-start | bytes 25165828
